TPU v7x, 512 devices: a whole 4x8x8 slice. The times are simulated.
512 devices in a mesh: grid: 64 (over y, z_hi, core), vec: 8 (over x, z_lo).
Axes of the slice: x: 4, y: 8, z: 8 (z_hi: 4, z_lo: 2; z = z_hi * 2 + z_lo), core: 2. Of those that a mesh axis runs over, the one named last changes fastest.
Arguments:
- tgt_coords: float32 [3, 8192], P(None, 'grid'), may hold values from 0 to 1
- src_coords: float32 [3, 8192], P(None, 'grid'), may hold values from 0 to 1
- src_values: float32 [2048, 8192], P('vec', 'grid'), may hold values from -0.26516503 to 0.26516503
- grad_vectors: float32 [3, 2048, 8192], P(None, 'vec', 'grid'), may hold values from -0.75 to 0.75
Outputs:
- interaction: float32 [2048, 2048], P('grid', 'vec')
All inputs are finite; a program needn't handle non-finite values.
Results may differ from a plain program's by a relative error of at most 0.00023.
Values sent between devices are 32-bit elements; how exact they have to be, the bound alone decides.
No kernel may reach another device: no remote copies, remote signals or barrier semaphores. Data moves between devices by JAX's collectives and lax.ppermute only.
A program may use at most 64 MiB of HBM per device.

v0:
```python
import math
import jax
import jax.numpy as jnp
from jax import lax
from jax.sharding import PartitionSpec as P

stiff = 1.0
soft = 0.05


def in_one_piece(arrays, axis, dim, along):
    ends, at = ([], 0)
    for a in arrays[:-1]:
        at += a.shape[along]
        ends.append(at)
    both = jnp.concatenate(arrays, axis=along)
    return tuple(jnp.split(lax.all_gather(both, axis, axis=dim, tiled=True), ends, axis=along))


def cut_along(array, dim, peers):
    shape = array.shape
    blocks = array.reshape(*shape[:dim], peers, shape[dim] // peers, *shape[dim + 1 :])
    return jnp.moveaxis(blocks, dim, 0)


def sum_at_owner(array, axis, dim):
    blocks = cut_along(array, dim, lax.axis_size(axis))
    arrived = lax.all_to_all(blocks, axis, split_axis=0, concat_axis=0, tiled=True)
    return arrived.sum(axis=0)


def pair_kernel(targets, sources):
    diff = targets[:, :, None] - sources[:, None, :]
    dist2 = jnp.sum(diff * diff, axis=0)
    scale = 0.5 / ((1.0 + stiff * jnp.sqrt(dist2)) ** 2 * jnp.sqrt(dist2 + soft * soft))
    return diff * scale[None, :, :]


def body(tgt_coords, src_coords, src_values, grad_vectors):
    width = src_values.shape[0]
    tgt_rows = tgt_coords.shape[1]
    gathered = lax.all_gather(grad_vectors, "vec", axis=1, tiled=True)
    start_sum = jnp.zeros((3, tgt_rows, width), jnp.float32)
    total = start_sum
    coords, values = in_one_piece((src_coords, src_values), "grid", 1, 0)
    count = coords.shape[1]
    block_len = math.gcd(count, 512)
    nblocks = count // block_len
    coord_blocks = coords.reshape(3, nblocks, block_len).transpose(1, 0, 2)
    value_blocks = values.reshape(width, nblocks, block_len).transpose(1, 0, 2)

    def inner(carry, items):
        cblock, vblock = items
        kern = pair_kernel(tgt_coords, cblock)
        carry = carry + jnp.einsum("cts,qs->ctq", kern, vblock, precision=lax.Precision.HIGHEST)
        return (carry, None)

    total, _ = lax.scan(inner, total, (coord_blocks, value_blocks))
    partial_value = jnp.einsum("cpt,ctq->pq", gathered, total, precision=lax.Precision.HIGHEST)
    return sum_at_owner(partial_value, "grid", 0)


def solution(mesh):
    return jax.shard_map(
        body,
        mesh=mesh,
        in_specs=(P(None, "grid"), P(None, "grid"), P("vec", "grid"), P(None, "vec", "grid")),
        out_specs=P("grid", "vec"),
        check_vma=False,
    )
```

profile of v0, /device:TPU:24, one launch (start us, length us, event | category | flops | bytes accessed | tf_op | source)
XLA Modules:
  0.0 294.5 jit_solution(4307227119990213914)
XLA Ops:
  9.9 126.4 %all-gather.3.cloned.1.call-done = f32[259,8192]{0,1:T(8,128)} async-done(((f32[259,128]{0,1:T(8,128)}), f32[259,8192]{0,1:T(8,128)}) %all-gather.3.cloned.1.call-update) | async-done | bytes 8486928 | tf_op jit(solution)/shard_map/all_gather | solution.py:17
  136.3 4.4 %split.8 = f32[3,8192]{0,1:T(8,128)} slice(f32[259,8192]{0,1:T(8,128)} %all-gather.3.cloned.1.call-done), slice={[0:3], [0:8192]} | slice | bytes 196608 | tf_op jit(solution)/shard_map/split | solution.py:17
  140.7 2.8 copy.8
  143.6 10.0 %split.9 = f32[256,8192]{0,1:T(8,128)} slice(f32[259,8192]{0,1:T(8,128)} %all-gather.3.cloned.1.call-done), slice={[3:259], [0:8192]} | slice | bytes 16777216 | tf_op jit(solution)/shard_map/split | solution.py:17
  153.6 38.8 %while.11 = (s32[]{:T(128)}, f32[3,128,256]{2,1,0:T(8,128)S(1)}, f32[3,128]{1,0:T(4,128)S(1)}, f32[16,3,512]{2,1,0:T(4,128)S(1)}, f32[16,256,512]{1,2,0:T(8,128)}, /*index=5*/s32[]{:T(128)}, s32[]{:T(128)}) while((s32[]{:T(128)}, f32[3,128,256]{2,1,0:T(8,128)S(1)}, f32[3,128]{1,0:T(4,128)S(1)}, f32[16,3,512]{2,1,0:T(4,128)S(1)}, ...), condition=%wide.region_2.3_spmd.clone, body=%wide.region_0.2_spmd.clone.sunk | while | flops 605421568 | bytes 2387047 | solution.py:58
  153.9 2.0 convolution_add_fusion.2
  156.3 2.1 convolution_add_fusion.2
  158.8 2.1 convolution_add_fusion.2
  161.2 2.0 convolution_add_fusion.2
  163.6 2.0 convolution_add_fusion.2
  166.1 2.0 convolution_add_fusion.2
  168.5 2.0 convolution_add_fusion.2
  170.9 2.0 convolution_add_fusion.2
  173.3 2.1 convolution_add_fusion.2
  175.8 2.1 convolution_add_fusion.2
  178.2 2.0 convolution_add_fusion.2
  180.6 2.0 convolution_add_fusion.2
  183.1 2.0 convolution_add_fusion.2
  185.5 2.0 convolution_add_fusion.2
  187.9 2.1 convolution_add_fusion.2
  190.4 2.1 convolution_add_fusion.2
  192.4 18.9 %all-gather.5.cloned.1.call-done = f32[3,2048,128]{2,1,0:T(8,128)} async-done(((f32[3,256,128]{2,1,0:T(8,128)}), f32[3,2048,128]{2,1,0:T(8,128)}) %all-gather.5.cloned.1.call-update) | async-done | bytes 3145744 | tf_op jit(solution)/shard_map/all_gather | solution.py:42
  211.3 7.1 %convolution_bitcast_fusion = f32[2048,256]{0,1:T(8,128)S(1)} fusion(f32[3,128,256]{2,1,0:T(8,128)S(1)} %get-tuple-element.32, f32[3,2048,128]{2,1,0:T(8,128)} %all-gather.5.cloned.1.call-done), kind=kOutput, calls=%fused_computation.12 | convolution fusion | flops 2415919104 | bytes 5636096 | tf_op jit(solution)/shard_map/cpt,ctq->pq/dot_general | solution.py:59
  220.3 66.6 %all_to_all.5 = f32[64,32,256]{2,1,0:T(8,128)S(1)} all-to-all(f32[64,32,256]{2,1,0:T(8,128)} %bitcast.25), channel_id=1, replica_groups=mesh['grid'=64,'vec'=8] {'grid'}, dimensions={0} | all-to-all | bytes 4194304 | tf_op jit(solution)/shard_map/all_to_all | solution.py:28
  (60 shorter events, 11.2 us)
Async XLA Ops:
  6.5 129.8 %all-gather.3.cloned.1.call-start = ((), (), s32[]{:S(2)}) async-start(), calls=%async_computation.1 | async-start | bytes 12779520 | tf_op jit(solution)/shard_map/all_gather | solution.py:17
  9.2 202.2 %all-gather.5.cloned.1.call-start = ((), (), s32[]{:S(2)}) async-start(), calls=%async_computation.2 | async-start | bytes 3538944 | tf_op jit(solution)/shard_map/all_gather | solution.py:42
  143.6 10.0 %copy-start = (f32[3,128]{1,0:T(4,128)S(1)}, f32[3,128]{1,0:T(4,128)}, u32[]{:S(2)}) copy-start(f32[3,128]{1,0:T(4,128)} %param.6) | copy-start | bytes 4612
Sparse Core Ops, SparseCore 0:
  10.6 125.6 all-gather.2
  138.4 72.8 all-gather.4
where the time goes:
time: 296 us; the launch traced here: 294 us
  waiting for transfers between devices  146 us (49%)
  blocking collectives  66.6 us (22%)
  matrix products  39.9 us (13%)
  local copies, waits for them, and re-layouts  21 us (7%)
  between operations  13.4 us (5%)
  other arithmetic  6.7 us (2%)
    all_gather x1, waiting for transfers between devices, in_one_piece(): lax.all_gather(both, axis, axis=dim, tiled=True)  126 us
    all_to_all x1, blocking collectives, sum_at_owner(): lax.all_to_all(blocks, axis, split_axis=0, concat_axis=0, tiled=True)  66.6 us
    dot_general x16, matrix products, inner(): jnp.einsum('cts,qs->ctq', kern, vblock, precision=lax.Precision.HIGHEST)  32.8 us
    all_gather x1, waiting for transfers between devices, body(): gathered = lax.all_gather(grad_vectors, 'vec', axis=1, tiled=True)  18.9 us
    split x2, local copies, waits for them, and re-layouts, in_one_piece(): jnp.split(lax.all_gather(both, axis, axis=dim, tiled=True), ends, axis=al...  14.4 us
    dot_general x1, matrix products, body(): jnp.einsum('cpt,ctq->pq', gathered, total, precision=lax.Precision.HIGHEST)  7.14 us
  transfers between devices with their start and end apart: 2, of which 2 were waited for; matrix products, arithmetic and copies ran while one was open for 19% of the time, Pallas kernels for 0%

commit v1 on v0

--- a/solution.py
+++ b/solution.py
@@ -39,7 +39,9 @@
 def body(tgt_coords, src_coords, src_values, grad_vectors):
     width = src_values.shape[0]
     tgt_rows = tgt_coords.shape[1]
-    gathered = lax.all_gather(grad_vectors, "vec", axis=1, tiled=True)
+    gathered = jnp.concatenate(
+        lax.all_to_all(jnp.stack([grad_vectors] * lax.axis_size("vec")), "vec", 0, 0), axis=1
+    )
     start_sum = jnp.zeros((3, tgt_rows, width), jnp.float32)
     total = start_sum
     coords, values = in_one_piece((src_coords, src_values), "grid", 1, 0)

time: 296 us -> 273 us (0.922)
  waiting for transfers between devices: 146 us -> 114 us
  local copies, waits for them, and re-layouts: 21 us -> 28 us
  starting transfers between devices: 0.04 us -> 6.11 us
  blocking collectives: 66.6 us -> 62.3 us
    all_gather x1, waiting for transfers between devices: 126 us -> 69.6 us  [in_one_piece(): lax.all_gather(both, axis, axis=dim, tiled=True)]
    all_to_all x0 -> x1, waiting for transfers between devices: none -> 44.6 us  [body(): lax.all_to_all(jnp.stack([grad_vectors] * lax.axis_size('vec')), 'vec', 0...]
    all_gather x1 -> x0, waiting for transfers between devices: 18.9 us -> none  [body(): gathered = lax.all_gather(grad_vectors, 'vec', axis=1, tiled=True)]
    all_to_all x0 -> x1, starting transfers between devices: none -> 6.11 us  [body(): lax.all_to_all(jnp.stack([grad_vectors] * lax.axis_size('vec')), 'vec', 0...]
    all_to_all x1, blocking collectives: 66.6 us -> 62.3 us  [sum_at_owner(): lax.all_to_all(blocks, axis, split_axis=0, concat_axis=0, tiled=True)]
    reshape x0 -> x1, local copies, waits for them, and re-layouts: none -> 3.87 us  [body(): jnp.concatenate(lax.all_to_all(jnp.stack([grad_vectors] * lax.axis_size('...]
    another operation x0 -> x1, local copies, waits for them, and re-layouts: none -> 2.99 us  [body(): jnp.stack([grad_vectors] * lax.axis_size('vec'))]
  transfers between devices with their start and end apart: 2 -> 2, of which waited for: 2 -> 2; matrix products, arithmetic and copies ran while one was open for 19% -> 3% of each run, Pallas kernels for 0% -> 0%
where the time goes in v1:
time: 273 us; the launch traced here: 271 us
  waiting for transfers between devices  114 us (42%)
  blocking collectives  62.3 us (23%)
  matrix products  39.9 us (15%)
  local copies, waits for them, and re-layouts  28 us (10%)
  between operations  13.4 us (5%)
  other arithmetic  6.7 us (2%)
  starting transfers between devices  6.11 us (2%)
    all_gather x1, waiting for transfers between devices, in_one_piece(): lax.all_gather(both, axis, axis=dim, tiled=True)  69.6 us
    all_to_all x1, blocking collectives, sum_at_owner(): lax.all_to_all(blocks, axis, split_axis=0, concat_axis=0, tiled=True)  62.3 us
    all_to_all x1, waiting for transfers between devices, body(): lax.all_to_all(jnp.stack([grad_vectors] * lax.axis_size('vec')), 'vec', 0...  44.6 us
    dot_general x16, matrix products, inner(): jnp.einsum('cts,qs->ctq', kern, vblock, precision=lax.Precision.HIGHEST)  32.8 us
    split x2, local copies, waits for them, and re-layouts, in_one_piece(): jnp.split(lax.all_gather(both, axis, axis=dim, tiled=True), ends, axis=al...  14.5 us
    dot_general x1, matrix products, body(): jnp.einsum('cpt,ctq->pq', gathered, total, precision=lax.Precision.HIGHEST)  7.14 us
    all_to_all x1, starting transfers between devices, body(): lax.all_to_all(jnp.stack([grad_vectors] * lax.axis_size('vec')), 'vec', 0...  6.11 us
  transfers between devices with their start and end apart: 2, of which 2 were waited for; matrix products, arithmetic and copies ran while one was open for 3% of the time, Pallas kernels for 0%

profile of v1, /device:TPU:24, one launch (start us, length us, event | category | flops | bytes accessed | tf_op | source)
XLA Modules:
  0.0 271.5 jit_solution(3213325539596021698)
XLA Ops:
  9.2 3.0 %stack.2 = f32[8,3,256,128]{3,2,1,0:T(8,128)} broadcast(f32[3,256,128]{2,1,0:T(8,128)} %param.9), dimensions={1,2,3} | broadcast | bytes 3538944 | tf_op jit(solution)/shard_map/stack | solution.py:43
  12.2 6.1 %all-to-all-start = ((f32[8,3,256,128]{3,2,1,0:T(8,128)}), f32[8,3,256,128]{3,2,1,0:T(8,128)}, u32[]{:S(2)}, u32[]{:S(2)}) async-start(f32[8,3,256,128]{3,2,1,0:T(8,128)} %stack.2), calls=%async_computation | async-start | bytes 6291456 | tf_op jit(solution)/shard_map/all_to_all | solution.py:43
  18.3 44.6 %all-to-all-done = f32[8,3,256,128]{3,2,1,0:T(8,128)} async-done(((f32[8,3,256,128]{3,2,1,0:T(8,128)}), f32[8,3,256,128]{3,2,1,0:T(8,128)}, u32[]{:S(2)}, u32[]{:S(2)}) %all-to-all-start) | async-done | bytes 3145760 | tf_op jit(solution)/shard_map/all_to_all | solution.py:43
  62.9 3.9 %copy.16 = f32[3,8,256,128]{3,2,1,0:T(8,128)} copy(f32[3,8,256,128]{3,2,0,1:T(8,128)} %bitcast.4) | data formatting | bytes 6291456 | tf_op jit(solution)/shard_map/reshape | solution.py:42
  66.8 69.6 %all-gather.2.cloned.1.call-done = f32[259,8192]{0,1:T(8,128)} async-done(((f32[259,128]{0,1:T(8,128)}), f32[259,8192]{0,1:T(8,128)}) %all-gather.2.cloned.1.call-update) | async-done | bytes 8486928 | tf_op jit(solution)/shard_map/all_gather | solution.py:17
  136.4 4.5 %split.8 = f32[3,8192]{0,1:T(8,128)} slice(f32[259,8192]{0,1:T(8,128)} %all-gather.2.cloned.1.call-done), slice={[0:3], [0:8192]} | slice | bytes 196608 | tf_op jit(solution)/shard_map/split | solution.py:17
  140.9 2.8 %copy.14 = f32[3,16,512]{2,0,1:T(4,128)S(1)} copy(f32[3,16,512]{0,2,1:T(8,128)} %bitcast.25) | data formatting | bytes 196608 | tf_op jit(solution)/shard_map/reshape | solution.py:51
  143.7 10.0 %split.9 = f32[256,8192]{0,1:T(8,128)} slice(f32[259,8192]{0,1:T(8,128)} %all-gather.2.cloned.1.call-done), slice={[3:259], [0:8192]} | slice | bytes 16777216 | tf_op jit(solution)/shard_map/split | solution.py:17
  153.8 38.8 %while.11 = (s32[]{:T(128)}, f32[3,128,256]{2,1,0:T(8,128)S(1)}, f32[3,128]{1,0:T(4,128)S(1)}, f32[16,3,512]{2,1,0:T(4,128)S(1)}, f32[16,256,512]{1,2,0:T(8,128)}, /*index=5*/s32[]{:T(128)}, s32[]{:T(128)}) while((s32[]{:T(128)}, f32[3,128,256]{2,1,0:T(8,128)S(1)}, f32[3,128]{1,0:T(4,128)S(1)}, f32[16,3,512]{2,1,0:T(4,128)S(1)}, ...), condition=%wide.region_2.3_spmd.clone, body=%wide.region_0.2_spmd.clone.sunk | while | flops 605421568 | bytes 2387047 | solution.py:60
  154.1 2.0 convolution_add_fusion.2
  156.5 2.0 convolution_add_fusion.2
  159.0 2.0 convolution_add_fusion.2
  161.4 2.0 convolution_add_fusion.2
  163.8 2.0 convolution_add_fusion.2
  166.2 2.0 convolution_add_fusion.2
  168.7 2.0 convolution_add_fusion.2
  171.1 2.0 convolution_add_fusion.2
  173.5 2.0 convolution_add_fusion.2
  176.0 2.0 convolution_add_fusion.2
  178.4 2.0 convolution_add_fusion.2
  180.8 2.0 convolution_add_fusion.2
  185.7 2.0 convolution_add_fusion.2
  192.6 7.1 %convolution_bitcast_fusion = f32[2048,256]{0,1:T(8,128)S(1)} fusion(f32[3,128,256]{2,1,0:T(8,128)S(1)} %get-tuple-element.32, f32[3,2048,128]{2,1,0:T(8,128)} %bitcast.27), kind=kOutput, calls=%fused_computation.12 | convolution fusion | flops 2415919104 | bytes 5636096 | tf_op jit(solution)/shard_map/cpt,ctq->pq/dot_general | solution.py:61
  201.6 62.3 %all_to_all.10 = f32[64,32,256]{2,1,0:T(8,128)S(1)} all-to-all(f32[64,32,256]{2,1,0:T(8,128)} %bitcast.28), channel_id=1, replica_groups=mesh['grid'=64,'vec'=8] {'grid'}, dimensions={0} | all-to-all | bytes 4194304 | tf_op jit(solution)/shard_map/all_to_all | solution.py:28
  (61 shorter events, 16.6 us)
Async XLA Ops:
  6.5 129.8 %all-gather.2.cloned.1.call-start = ((), (), s32[]{:S(2)}) async-start(), calls=%async_computation.2 | async-start | bytes 12779520 | tf_op jit(solution)/shard_map/all_gather | solution.py:17
  12.2 50.7 %all-to-all-start = ((f32[8,3,256,128]{3,2,1,0:T(8,128)}), f32[8,3,256,128]{3,2,1,0:T(8,128)}, u32[]{:S(2)}, u32[]{:S(2)}) async-start(f32[8,3,256,128]{3,2,1,0:T(8,128)} %stack.2), calls=%async_computation | async-start | bytes 6291456 | tf_op jit(solution)/shard_map/all_to_all | solution.py:43
  143.7 10.0 %copy-start = (f32[3,128]{1,0:T(4,128)S(1)}, f32[3,128]{1,0:T(4,128)}, u32[]{:S(2)}) copy-start(f32[3,128]{1,0:T(4,128)} %param.6) | copy-start | bytes 4612
Sparse Core Ops, SparseCore 0:
  10.6 125.6 all-gather.1
